TPU v7x, 256 devices: a whole 4x4x8 slice. The times are simulated.
256 devices in a mesh: row: 16 (over x, z_lo, core), col: 16 (over y, z_hi).
Axes of the slice: x: 4, y: 4, z: 8 (z_hi: 4, z_lo: 2; z = z_hi * 2 + z_lo), core: 2. Of those that a mesh axis runs over, the one named last changes fastest.
Arguments:
- dosage: bfloat16 [1536, 196608], P(None, ('row', 'col')), may hold values from 0 to 2
- zscores: bfloat16 [196608], P(('row', 'col')), may hold values from -18 to 18
- band_reach: int32 [256], replicated, may hold values from 0 to 2, as said below
Outputs:
- ld_tiles: bfloat16 [196608, 3840], P(('row', 'col'))
- smoothed: float32 [196608], P(('row', 'col'))
- quadratic: float32 [], replicated
Inputs may be any that keep to these rules, and one draw needn't show every extreme that they name: `band_reach`: the first 3 blocks, the last 3 blocks and some two neighbouring blocks reach 2.
All inputs are finite; a program needn't handle non-finite values.
Results may differ from a plain program's by a relative error of at most 0.0042.
Values may be sent and summed in bfloat16 or wider, within the bound.
A program may use at most 64 MiB of HBM per device.

v0:
```python
import jax
import jax.numpy as jnp
from jax import lax
from jax.sharding import Mesh
from jax.sharding import PartitionSpec as P

BAND = 2
ROW_COL = ("row_0", "row_1", "row_2", "col_0", "col_1")


def passed_along(value, axis, steps):
    count = lax.axis_size(axis)
    initial, last = (max(0, -steps), min(count, count - steps))
    return lax.ppermute(value, axis, [(source, source + steps) for source in range(initial, last)])


def by_axis(value, axes):
    for axis in axes:
        value = lax.psum(value, axis)
    return value


def standardize(dosage):
    values = dosage.astype(jnp.float32)
    column_mean = jnp.mean(values, axis=0)
    centered = values - column_mean
    variance = jnp.mean(centered * centered, axis=0)
    return (centered * lax.rsqrt(variance + 1e-05)).astype(jnp.bfloat16)


def body(dosage, zscores, band_reach):
    samples = dosage.shape[0]
    block_width = zscores.shape[0]
    block_count = lax.axis_size(ROW_COL)
    position = lax.axis_index(ROW_COL)
    scaled = standardize(dosage)
    own_reach = lax.dynamic_index_in_dim(band_reach, position, 0, False)

    def allowed(offset):
        other = position + offset
        inside = (other >= 0) & (other < block_count)
        their_reach = lax.dynamic_index_in_dim(
            band_reach, jnp.clip(other, 0, block_count - 1), 0, False
        )
        return inside & (abs(offset) <= jnp.minimum(own_reach, their_reach))

    def make_tile(left, right, offset):
        product = (
            lax.dot_general(
                left, right, (((0,), (0,)), ((), ())), preferred_element_type=jnp.float32
            )
            / samples
        )
        return jnp.where(allowed(offset), product, 0.0).astype(jnp.bfloat16)

    def apply_tile(ld_tile, near_scores):
        return jnp.dot(ld_tile, near_scores, preferred_element_type=jnp.float32)

    own_z = zscores.astype(jnp.float32)
    tile_map = {0: make_tile(scaled, scaled, 0)}
    score_map = {0: zscores}
    for offset in range(1, BAND + 1):
        far_scaled, far_z = passed_along((scaled, zscores), ROW_COL, -offset)
        tile_map[offset] = make_tile(scaled, far_scaled, offset)
        score_map[offset] = far_z
    terms = {}
    for offset in range(0, BAND + 1):
        terms[offset] = apply_tile(tile_map[offset], score_map[offset])
    total = None
    for offset in range(1, BAND + 1):
        returned, returned_z = passed_along((tile_map[offset], zscores), ROW_COL, offset)
        tile_map[-offset] = returned.T
        score_map[-offset] = returned_z
    for offset in range(1, BAND + 1):
        terms[-offset] = apply_tile(tile_map[-offset], score_map[-offset])
    smoothed = terms[0]
    for offset in range(1, BAND + 1):
        smoothed = smoothed + terms[offset] + terms[-offset]
    total = by_axis(jnp.sum(own_z * smoothed), ROW_COL)
    quadratic = total / (block_count * block_width)
    ld_tiles = jnp.concatenate([tile_map[offset] for offset in range(-BAND, BAND + 1)], axis=1)
    return (ld_tiles, smoothed, quadratic)


def solution(mesh):
    torus = Mesh(mesh.devices.reshape(4, 2, 2, 4, 4), ("row_0", "row_1", "row_2", "col_0", "col_1"))
    return jax.shard_map(
        body,
        mesh=torus,
        in_specs=(P(None, ROW_COL), P(ROW_COL), P()),
        out_specs=(P(ROW_COL, None), P(ROW_COL), P()),
        check_vma=False,
    )
```

profile of v0, /device:TPU:1, one launch (start us, length us, event | category | flops | bytes accessed | tf_op | source)
XLA Modules:
  0.0 391.0 jit_solution(10155190319292497556)
XLA Ops:
  0.6 2.2 convert_reduce_fusion
  3.7 2.0 fusion.3
  5.7 11.7 %collective-permute-start.2 = (bf16[1536,768]{1,0:T(8,128)(2,1)}, bf16[1536,768]{1,0:T(8,128)(2,1)S(1)}, u32[]{:S(2)}, u32[]{:S(2)}) collective-permute-start(bf16[1536,768]{1,0:T(8,128)(2,1)} %fusion.3), channel_id=1, source_target_pairs={{1,0},{2,1},{3,2},{4,3},{5,4},{6,5},{7,6},{8,7},{9,8},{10,9},{11,1... | collective-permute-start | bytes 7077896 | tf_op jit(solution)/shard_map/ppermute | solution.py:14
  17.5 2.8 collective-permute-start
  23.3 90.2 %collective-permute-done.2 = bf16[1536,768]{1,0:T(8,128)(2,1)S(1)} collective-permute-done((bf16[1536,768]{1,0:T(8,128)(2,1)}, bf16[1536,768]{1,0:T(8,128)(2,1)S(1)}, u32[]{:S(2)}, u32[]{:S(2)}) %collective-permute-start.2) | collective-permute-done | bytes 2359328 | tf_op jit(solution)/shard_map/ppermute | solution.py:14
  113.5 3.7 select_convert_fusion.1
  117.2 8.6 %collective-permute-start.3 = (bf16[768,768]{0,1:T(8,128)(2,1)S(1)}, bf16[768,768]{0,1:T(8,128)(2,1)S(1)}, u32[]{:S(2)}, u32[]{:S(2)}) collective-permute-start(bf16[768,768]{0,1:T(8,128)(2,1)S(1)} %select_convert_fusion.1), channel_id=1, source_target_pairs={{0,1},{1,2},{2,3},{3,4},{4,5},{5,6},{6,7},{7,8},{8,9},{9,10},{10,1... | collective-permute-start | bytes 3538952 | tf_op jit(solution)/shard_map/ppermute | solution.py:14
  125.8 4.4 %select_convert_fusion.2 = bf16[768,768]{0,1:T(8,128)(2,1)S(1)} fusion(bf16[1536,768]{1,0:T(8,128)(2,1)} %fusion.3, bf16[1536,768]{1,0:T(8,128)(2,1)} %collective-permute-done, pred[]{:T(512)S(6)} %and.24), kind=kOutput, calls=%fused_computation.8 | convolution fusion | flops 1813708800 | bytes 5898241 | tf_op jit(solution)/shard_map/dot_general | solution.py:49
  131.7 106.1 %collective-permute-start.1 = (bf16[768,768]{1,0:T(8,128)(2,1)}, bf16[768,768]{1,0:T(8,128)(2,1)}, u32[]{:S(2)}, u32[]{:S(2)}) collective-permute-start(bf16[768,768]{1,0:T(8,128)(2,1)} %copy.6), channel_id=1, source_target_pairs={{0,2},{1,3},{2,4},{3,5},{4,6},{5,7},{6,8},{7,9},{8,10},{9,11},{10,... | collective-permute-start | bytes 3538952 | tf_op jit(solution)/shard_map/ppermute | solution.py:14
  237.9 1.9 collective-permute-start.6
  239.8 1.9 collective-permute-start.5
  241.7 7.9 %collective-permute-start.4 = (bf16[768]{0:T(1024)(128)(2,1)S(1)}, bf16[768]{0:T(1024)(128)(2,1)}, u32[]{:S(2)}, u32[]{:S(2)}) collective-permute-start(bf16[768]{0:T(1024)(128)(2,1)S(1)} %copy-done.3), channel_id=1, source_target_pairs={{1,0},{2,1},{3,2},{4,3},{5,4},{6,5},{7,6},{8,7},{9,8},{10,9},{11,1... | collective-permute-start | bytes 4616 | tf_op jit(solution)/shard_map/ppermute | solution.py:14
  249.6 55.9 %collective-permute-done.6 = bf16[768]{0:T(1024)(128)(2,1)S(1)} collective-permute-done((bf16[768]{0:T(1024)(128)(2,1)S(1)}, bf16[768]{0:T(1024)(128)(2,1)S(1)}, u32[]{:S(2)}, u32[]{:S(2)}) %collective-permute-start.6) | collective-permute-done | bytes 1568 | tf_op jit(solution)/shard_map/ppermute | solution.py:14
  305.5 1.9 collective-permute-start.7
  309.3 7.2 %collective-permute-done.7 = bf16[768]{0:T(1024)(128)(2,1)} collective-permute-done((bf16[768]{0:T(1024)(128)(2,1)S(1)}, bf16[768]{0:T(1024)(128)(2,1)}, u32[]{:S(2)}, u32[]{:S(2)}) %collective-permute-start.7) | collective-permute-done | bytes 1568 | tf_op jit(solution)/shard_map/ppermute | solution.py:14
  319.8 2.5 bitcast_dynamic-update-slice_fusion
  323.4 5.4 %constant_dynamic-update-slice_fusion.2 = (bf16[768,3840]{0,1:T(8,128)(2,1)}, bf16[768,768]{0,1:T(8,128)(2,1)S(1)}) fusion(bf16[768,3840]{0,1:T(8,128)(2,1)} %constant_dynamic-update-slice_fusion.3, bf16[1536,768]{1,0:T(8,128)(2,1)} %fusion.3, pred[]{:T(512)S(6)} %and.28), kind=kOutput, calls=%fused_computation.19 | convolution fusion | flops 1813708800 | bytes 7077889 | tf_op jit(solution)/shard_map/dot_general | solution.py:49
  329.6 1.6 fusion.6
  332.4 15.4 %psum.35 = f32[]{:T(128)} all-reduce(f32[]{:T(128)} %get-tuple-element.6), channel_id=1, replica_groups=mesh['row_0'=4,'row_1'=2,'row_2'=2,'col_0'=4,'col_1'=4] {'row_0'}, use_global_device_ids=true, to_apply=%region_3.4 | all-reduce | flops 1 | bytes 8 | tf_op jit(solution)/shard_map/psum | solution.py:19
  347.8 4.4 %psum.36 = f32[]{:T(128)} all-reduce(f32[]{:T(128)} %psum.35), channel_id=1, replica_groups=mesh['row_0'=4,'row_1'=2,'row_2'=2,'col_0'=4,'col_1'=4] {'row_1'}, use_global_device_ids=true, to_apply=%region_4.5 | all-reduce | flops 1 | bytes 8 | tf_op jit(solution)/shard_map/psum | solution.py:19
  353.2 7.4 %psum.37 = f32[]{:T(128)} all-reduce(f32[]{:T(128)} %psum.36), channel_id=1, replica_groups=mesh['row_0'=4,'row_1'=2,'row_2'=2,'col_0'=4,'col_1'=4] {'row_2'}, use_global_device_ids=true, to_apply=%region_5.6 | all-reduce | flops 1 | bytes 8 | tf_op jit(solution)/shard_map/psum | solution.py:19
  361.7 6.7 %psum.38 = f32[]{:T(128)} all-reduce(f32[]{:T(128)} %psum.37), channel_id=1, replica_groups=mesh['row_0'=4,'row_1'=2,'row_2'=2,'col_0'=4,'col_1'=4] {'col_0'}, use_global_device_ids=true, to_apply=%region_6.7 | all-reduce | flops 1 | bytes 8 | tf_op jit(solution)/shard_map/psum | solution.py:19
  368.4 8.4 %copy.8 = bf16[768,3840]{1,0:T(8,128)(2,1)} copy(bf16[768,3840]{0,1:T(8,128)(2,1)} %constant_dynamic-update-slice_fusion) | data formatting | bytes 11796480
  376.8 12.4 %psum.39 = f32[]{:T(128)} all-reduce(f32[]{:T(128)} %psum.38), channel_id=1, replica_groups=mesh['row_0'=4,'row_1'=2,'row_2'=2,'col_0'=4,'col_1'=4] {'col_1'}, use_global_device_ids=true, to_apply=%region_7.8 | all-reduce | flops 1 | bytes 8 | tf_op jit(solution)/shard_map/psum | solution.py:19
  (36 shorter events, 12.1 us)
Async XLA Ops:
  0.6 2.4 copy-start
  3.7 16.6 %copy-start.5 = (s32[256]{0:T(256)S(1)}, s32[256]{0:T(256)}, u32[]{:S(2)}) copy-start(s32[256]{0:T(256)} %param.5) | copy-start | bytes 3076
  5.7 107.8 %collective-permute-start.2 = (bf16[1536,768]{1,0:T(8,128)(2,1)}, bf16[1536,768]{1,0:T(8,128)(2,1)S(1)}, u32[]{:S(2)}, u32[]{:S(2)}) collective-permute-start(bf16[1536,768]{1,0:T(8,128)(2,1)} %fusion.3), channel_id=1, source_target_pairs={{1,0},{2,1},{3,2},{4,3},{5,4},{6,5},{7,6},{8,7},{9,8},{10,9},{11,1... | collective-permute-start | bytes 7077896 | tf_op jit(solution)/shard_map/ppermute | solution.py:14
  17.5 108.3 %collective-permute-start = (bf16[1536,768]{1,0:T(8,128)(2,1)}, bf16[1536,768]{1,0:T(8,128)(2,1)}, u32[]{:S(2)}, u32[]{:S(2)}) collective-permute-start(bf16[1536,768]{1,0:T(8,128)(2,1)} %fusion.3), channel_id=1, source_target_pairs={{2,0},{3,1},{4,2},{5,3},{6,4},{7,5},{8,6},{9,7},{10,8},{11,9},{12,... | collective-permute-start | bytes 7077896 | tf_op jit(solution)/shard_map/ppermute | solution.py:14
  117.2 201.1 %collective-permute-start.3 = (bf16[768,768]{0,1:T(8,128)(2,1)S(1)}, bf16[768,768]{0,1:T(8,128)(2,1)S(1)}, u32[]{:S(2)}, u32[]{:S(2)}) collective-permute-start(bf16[768,768]{0,1:T(8,128)(2,1)S(1)} %select_convert_fusion.1), channel_id=1, source_target_pairs={{0,1},{1,2},{2,3},{3,4},{4,5},{5,6},{6,7},{7,8},{8,9},{9,10},{10,1... | collective-permute-start | bytes 3538952 | tf_op jit(solution)/shard_map/ppermute | solution.py:14
  130.2 107.6 %copy-start.3 = (bf16[768]{0:T(1024)(128)(2,1)S(1)}, bf16[768]{0:T(1024)(128)(2,1)}, u32[]{:S(2)}) copy-start(bf16[768]{0:T(1024)(128)(2,1)} %param.4) | copy-start | bytes 4612
  131.7 188.1 %collective-permute-start.1 = (bf16[768,768]{1,0:T(8,128)(2,1)}, bf16[768,768]{1,0:T(8,128)(2,1)}, u32[]{:S(2)}, u32[]{:S(2)}) collective-permute-start(bf16[768,768]{1,0:T(8,128)(2,1)} %copy.6), channel_id=1, source_target_pairs={{0,2},{1,3},{2,4},{3,5},{4,6},{5,7},{6,8},{7,9},{8,10},{9,11},{10,... | collective-permute-start | bytes 3538952 | tf_op jit(solution)/shard_map/ppermute | solution.py:14
  237.9 67.6 %collective-permute-start.6 = (bf16[768]{0:T(1024)(128)(2,1)S(1)}, bf16[768]{0:T(1024)(128)(2,1)S(1)}, u32[]{:S(2)}, u32[]{:S(2)}) collective-permute-start(bf16[768]{0:T(1024)(128)(2,1)S(1)} %copy-done.3), channel_id=1, source_target_pairs={{2,0},{3,1},{4,2},{5,3},{6,4},{7,5},{8,6},{9,7},{10,8},{11,9},{12,... | collective-permute-start | bytes 4616 | tf_op jit(solution)/shard_map/ppermute | solution.py:14
  239.8 68.9 %collective-permute-start.5 = (bf16[768]{0:T(1024)(128)(2,1)S(1)}, bf16[768]{0:T(1024)(128)(2,1)S(1)}, u32[]{:S(2)}, u32[]{:S(2)}) collective-permute-start(bf16[768]{0:T(1024)(128)(2,1)S(1)} %copy-done.3), channel_id=1, source_target_pairs={{0,1},{1,2},{2,3},{3,4},{4,5},{5,6},{6,7},{7,8},{8,9},{9,10},{10,1... | collective-permute-start | bytes 4616 | tf_op jit(solution)/shard_map/ppermute | solution.py:14
  241.7 67.0 %collective-permute-start.4 = (bf16[768]{0:T(1024)(128)(2,1)S(1)}, bf16[768]{0:T(1024)(128)(2,1)}, u32[]{:S(2)}, u32[]{:S(2)}) collective-permute-start(bf16[768]{0:T(1024)(128)(2,1)S(1)} %copy-done.3), channel_id=1, source_target_pairs={{1,0},{2,1},{3,2},{4,3},{5,4},{6,5},{7,6},{8,7},{9,8},{10,9},{11,1... | collective-permute-start | bytes 4616 | tf_op jit(solution)/shard_map/ppermute | solution.py:14
  305.5 11.0 %collective-permute-start.7 = (bf16[768]{0:T(1024)(128)(2,1)S(1)}, bf16[768]{0:T(1024)(128)(2,1)}, u32[]{:S(2)}, u32[]{:S(2)}) collective-permute-start(bf16[768]{0:T(1024)(128)(2,1)S(1)} %copy-done.3), channel_id=1, source_target_pairs={{0,2},{1,3},{2,4},{3,5},{4,6},{5,7},{6,8},{7,9},{8,10},{9,11},{10,... | collective-permute-start | bytes 4616 | tf_op jit(solution)/shard_map/ppermute | solution.py:14
  319.8 2.5 copy-start.1
  328.8 0.8 copy-start.2
  328.8 2.3 copy-start.4
where the time goes:
time: 395 us; the launch traced here: 391 us
  waiting for transfers between devices  153 us (39%)
  starting transfers between devices  143 us (36%)
  blocking collectives  46.2 us (12%)
  local copies, waits for them, and re-layouts  19.8 us (5%)
  matrix products  16.4 us (4%)
  between operations  6.29 us (2%)
  other arithmetic  6.11 us (2%)
    ppermute x8, waiting for transfers between devices, passed_along(): lax.ppermute(value, axis, [(source, source + steps) for source in range(i...  153 us
    ppermute x8, starting transfers between devices, passed_along(): lax.ppermute(value, axis, [(source, source + steps) for source in range(i...  143 us
    psum x5, blocking collectives, by_axis(): value = lax.psum(value, axis)  46.2 us
    dot_general x3, matrix products, make_tile(): lax.dot_general(left, right, (((0,), (0,)), ((), ())), preferred_element_...  13.6 us
    unnamed x17, local copies, waits for them, and re-layouts  13.2 us
  transfers between devices with their start and end apart: 8, of which 3 were waited for; matrix products, arithmetic and copies ran while one was open for 4% of the time, Pallas kernels for 0%

commit v1 on v0

v1 whole, which is shorter than its diff:
```python
import functools

import jax
import jax.numpy as jnp
from jax import lax
from jax.experimental import pallas as pl
from jax.experimental.pallas import tpu as pltpu
from jax.sharding import Mesh
from jax.sharding import PartitionSpec as P

BAND = 2
MESH = pl.DeviceIdType.MESH
CHUNK = 256
STEP = 128
NT = (((1,), (1,)), ((), ()))

GROUPS = (((64, 4),), ((4, 4),), ((16, 2),), ((32, 2), (1, 4)))


def group_members(me, group):
    place, base = 0, me
    for stride, size in group:
        digit = lax.rem(lax.div(me, stride), size)
        base = base - digit * stride
        place = place * size + digit
    total = 1
    for _, size in group:
        total *= size

    def device(index):
        result = base
        for stride, size in reversed(group):
            result = result + lax.rem(index, size) * stride
            index = lax.div(index, size)
        return result

    return place, total, device


def column_stats(source, columns, samples):
    width = columns.size

    def add(step, total):
        rows = pl.ds(pl.multiple_of(step * STEP, STEP), STEP)
        values = source[rows, columns].astype(jnp.float32)
        return total + values.reshape(STEP // 8, 8, width).sum(axis=0)

    zero = jnp.zeros((8, width), jnp.float32)
    total = lax.fori_loop(0, samples // STEP, add, zero)
    mean = jnp.sum(total, axis=0, keepdims=True) / samples

    def add_square(step, total):
        rows = pl.ds(pl.multiple_of(step * STEP, STEP), STEP)
        centered = source[rows, columns].astype(jnp.float32) - mean
        return total + (centered * centered).reshape(STEP // 8, 8, width).sum(axis=0)

    total = lax.fori_loop(0, samples // STEP, add_square, zero)
    variance = jnp.sum(total, axis=0, keepdims=True) / samples
    return mean, lax.rsqrt(variance + 1e-05)


def standardize(source, plain, turned, columns, samples):
    mean, inverse = column_stats(source, columns, samples)

    def write(step, carry):
        rows = pl.ds(pl.multiple_of(step * STEP, STEP), STEP)
        values = (source[rows, columns].astype(jnp.float32) - mean) * inverse
        plain[rows, columns] = values.astype(jnp.bfloat16)
        turned[columns, rows] = values.T.astype(jnp.bfloat16)
        return carry

    lax.fori_loop(0, samples // STEP, write, 0)


def kernel(
    count,
    x_hbm,
    z_ref,
    reach_ref,
    out_hbm,
    smooth_ref,
    quad_ref,
    own,
    rx,
    plain,
    turned,
    middle,
    tx,
    near_z,
    tx_smooth,
    rx_smooth,
    partial,
    slots,
    load_sem,
    send_sem,
    recv_sem,
    z_send,
    z_recv,
    tile_send,
    tile_recv,
    smooth_send,
    smooth_recv,
    sum_send,
    sum_recv,
    store_sem,
):
    me = lax.axis_index("i")
    samples, width = x_hbm.shape
    chunks = width // CHUNK
    left, right = lax.rem(me + count - 1, count), lax.rem(me + 1, count)
    sides = (left, right)
    groups = [group_members(me, group) for group in GROUPS]

    barrier = pltpu.get_barrier_semaphore()
    greeted = 0
    for device in sides:
        pl.semaphore_signal(barrier, inc=1, device_id=(device,), device_id_type=MESH)
        greeted += 1
    for place, total, device in groups:
        for step in range(1, total):
            peer = device(lax.rem(place + step, total))
            pl.semaphore_signal(barrier, inc=1, device_id=(peer,), device_id_type=MESH)
            greeted += 1
    pl.semaphore_wait(barrier, greeted)

    load = pltpu.make_async_copy(x_hbm, own, load_sem)
    load.start()
    pending = []
    chunk_copies = []
    z_copies = []
    for side in range(2):
        copy = pltpu.make_async_remote_copy(
            src_ref=z_ref,
            dst_ref=near_z.at[1 - side],
            send_sem=z_send.at[side],
            recv_sem=z_recv.at[1 - side],
            device_id=(sides[side],),
            device_id_type=MESH,
        )
        copy.start()
        z_copies.append(copy)
    for chunk in range(chunks):
        columns = pl.ds(chunk * CHUNK, CHUNK)
        pair = []
        for side in range(2):
            copy = pltpu.make_async_remote_copy(
                src_ref=x_hbm.at[:, columns],
                dst_ref=rx.at[1 - side, :, columns],
                send_sem=send_sem.at[side, chunk],
                recv_sem=recv_sem.at[1 - side, chunk],
                device_id=(sides[side],),
                device_id_type=MESH,
            )
            copy.start()
            pair.append(copy)
        chunk_copies.append(pair)

    def reach_of(block):
        inside = (block >= 0) & (block < count)
        value = reach_ref[jnp.clip(block, 0, count - 1)]
        return jnp.where(inside, value, -1)

    def factor(first, second, offset):
        allowed = jnp.minimum(reach_of(first), reach_of(second)) >= offset
        return jnp.where(allowed, jnp.float32(1.0), jnp.float32(0.0)) / samples

    near_factor = (factor(me, me - 1, 1), factor(me, me + 1, 1))
    far_factor = factor(me - 1, me + 1, 2)
    own_factor = factor(me, me, 0)

    load.wait()
    for chunk in range(chunks):
        standardize(own, plain.at[2], turned.at[2], pl.ds(chunk * CHUNK, CHUNK), samples)

    def into_middle(slot, columns, place, scale):
        def rows_of(step, carry):
            rows = pl.ds(pl.multiple_of(step * CHUNK, CHUNK), CHUNK)
            product = jnp.dot(
                turned[2, rows, :], plain[slot, :, columns], preferred_element_type=jnp.float32
            )
            middle[rows, place] = (product * scale).astype(jnp.bfloat16)
            return carry

        lax.fori_loop(0, width // CHUNK, rows_of, 0)

    def stored(place, index):
        copy = pltpu.make_async_copy(
            middle.at[:, place],
            out_hbm.at[:, pl.ds(width + place.start, place.size)],
            store_sem.at[index],
        )
        copy.start()
        return copy

    for chunk in range(chunks):
        into_middle(
            2, pl.ds(chunk * CHUNK, CHUNK), pl.ds(width + chunk * CHUNK, CHUNK), own_factor
        )
    stores = [stored(pl.ds(width, width), 1)]

    def tile_copy(side, index, rows, columns):
        place = 4 * width if side == 0 else 0
        return pltpu.make_async_remote_copy(
            src_ref=tx.at[side, rows, columns],
            dst_ref=out_hbm.at[rows, pl.ds(place + columns.start, columns.size)],
            send_sem=tile_send.at[side, index],
            recv_sem=tile_recv.at[1 - side, index],
            device_id=(sides[side],),
            device_id_type=MESH,
        )

    tile_copies = []
    held_back = []
    for chunk in range(chunks):
        columns = pl.ds(chunk * CHUNK, CHUNK)
        for side in range(2):
            chunk_copies[chunk][1 - side].wait_recv()
            standardize(rx.at[side], plain.at[side], turned.at[side], columns, samples)
        pieces = [(columns, pl.ds(0, (chunk + 1) * CHUNK))]
        if chunk:
            pieces.append((pl.ds(0, chunk * CHUNK), columns))
        for index, (rows, across) in enumerate(pieces):
            for side in range(2):
                product = jnp.dot(
                    turned[side, rows, :],
                    plain[1 - side, :, across],
                    preferred_element_type=jnp.float32,
                )
                tx[side, rows, across] = (product * far_factor).astype(jnp.bfloat16)
        for side in range(2):
            into_middle(
                side,
                columns,
                pl.ds(2 * width * side + chunk * CHUNK, CHUNK),
                near_factor[side],
            )
        for index, (rows, across) in enumerate(pieces):
            for side in range(2):
                copy = tile_copy(side, 2 * chunk + index, rows, across)
                tile_copies.append(copy)
                if chunk == chunks - 1 and index == 1:
                    held_back.append(copy)
                else:
                    copy.start()
    stores.append(stored(pl.ds(0, width), 0))
    stores.append(stored(pl.ds(2 * width, width), 2))

    def applied(scores, tile):
        scores = jnp.broadcast_to(scores, (8, width)).astype(jnp.bfloat16)
        return lax.dot_general(scores, tile, NT, preferred_element_type=jnp.float32)[0:1, :]

    own_z = z_ref[...]
    for side in range(2):
        z_copies[side].wait_recv()
    smooth_own = applied(own_z, middle[:, pl.ds(width, width)])
    smooth_left = applied(near_z[0], middle[:, pl.ds(0, width)])
    smooth_right = applied(near_z[1], middle[:, pl.ds(2 * width, width)])
    for side in range(2):
        tx_smooth[side] = applied(near_z[1 - side], tx[side])

    share = own_z * (smooth_own + 2.0 * smooth_right) + 2.0 * near_z[0] * tx_smooth[0]
    total = jnp.sum(share, axis=1, keepdims=True)
    partial[0] = jnp.broadcast_to(total, (8, 128))

    smooth_copies = []
    sum_copies = []
    first_slot = 0
    for index, (place, size, device) in enumerate(groups):
        slots[first_slot + place] = partial[index]
        copies = []
        for step in range(1, size):
            peer = device(lax.rem(place + step, size))
            copy = pltpu.make_async_remote_copy(
                src_ref=partial.at[index],
                dst_ref=slots.at[first_slot + place],
                send_sem=sum_send.at[first_slot + step],
                recv_sem=sum_recv.at[first_slot + step],
                device_id=(peer,),
                device_id_type=MESH,
            )
            copy.start()
            copies.append(copy)
        sum_copies += copies
        if index == len(groups) - 1:
            for side in range(2):
                copy = pltpu.make_async_remote_copy(
                    src_ref=tx_smooth.at[side],
                    dst_ref=rx_smooth.at[1 - side],
                    send_sem=smooth_send.at[side],
                    recv_sem=smooth_recv.at[1 - side],
                    device_id=(sides[side],),
                    device_id_type=MESH,
                )
                copy.start()
                smooth_copies.append(copy)
            for copy in held_back:
                copy.start()
        for copy in copies:
            copy.wait_recv()
        result = slots[first_slot]
        for slot in range(1, size):
            result = result + slots[first_slot + slot]
        if index == len(groups) - 1:
            quad_ref[...] = result / (count * width)
        else:
            partial[index + 1] = result
        first_slot += size

    for copy in smooth_copies:
        copy.wait_recv()
    smooth_ref[...] = (
        smooth_own + smooth_left + smooth_right + rx_smooth[0] + rx_smooth[1]
    )
    for copy in tile_copies:
        copy.wait_recv()
    for store in stores:
        store.wait()
    for pair in chunk_copies:
        for copy in pair:
            copy.wait_send()
    for copy in z_copies + tile_copies + smooth_copies + sum_copies:
        copy.wait_send()


def body(count, dosage, zscores, band_reach):
    samples, width = dosage.shape
    chunks = width // CHUNK
    slots = sum(functools.reduce(lambda a, b: a * b[1], group, 1) for group in GROUPS)
    bf16, f32 = jnp.bfloat16, jnp.float32
    vmem = pl.BlockSpec(memory_space=pltpu.VMEM)
    hbm = pl.BlockSpec(memory_space=pl.ANY)
    ld_tiles, smoothed, quadratic = pl.pallas_call(
        functools.partial(kernel, count),
        out_shape=(
            jax.ShapeDtypeStruct((width, (2 * BAND + 1) * width), bf16),
            jax.ShapeDtypeStruct((1, width), f32),
            jax.ShapeDtypeStruct((8, 128), f32),
        ),
        in_specs=[hbm, vmem, pl.BlockSpec(memory_space=pltpu.SMEM)],
        out_specs=(hbm, vmem, vmem),
        scratch_shapes=[
            pltpu.VMEM((samples, width), bf16),
            pltpu.VMEM((2, samples, width), bf16),
            pltpu.VMEM((3, samples, width), bf16),
            pltpu.VMEM((3, width, samples), bf16),
            pltpu.VMEM((width, 3 * width), bf16),
            pltpu.VMEM((2, width, width), bf16),
            pltpu.VMEM((2, 1, width), f32),
            pltpu.VMEM((2, 1, width), f32),
            pltpu.VMEM((2, 1, width), f32),
            pltpu.VMEM((len(GROUPS), 8, 128), f32),
            pltpu.VMEM((slots, 8, 128), f32),
            pltpu.SemaphoreType.DMA,
            pltpu.SemaphoreType.DMA((2, chunks)),
            pltpu.SemaphoreType.DMA((2, chunks)),
            pltpu.SemaphoreType.DMA((2,)),
            pltpu.SemaphoreType.DMA((2,)),
            pltpu.SemaphoreType.DMA((2, 2 * chunks)),
            pltpu.SemaphoreType.DMA((2, 2 * chunks)),
            pltpu.SemaphoreType.DMA((2,)),
            pltpu.SemaphoreType.DMA((2,)),
            pltpu.SemaphoreType.DMA((slots,)),
            pltpu.SemaphoreType.DMA((slots,)),
            pltpu.SemaphoreType.DMA((3,)),
        ],
        compiler_params=pltpu.CompilerParams(
            collective_id=0, has_side_effects=True, vmem_limit_bytes=60 * 1024 * 1024
        ),
    )(dosage, zscores.astype(f32).reshape(1, width), band_reach)
    return ld_tiles, smoothed.reshape(width), quadratic[0, 0]


def solution(mesh):
    count = mesh.devices.size
    line = Mesh(mesh.devices.reshape(count), ("i",))
    return jax.shard_map(
        functools.partial(body, count),
        mesh=line,
        in_specs=(P(None, "i"), P("i"), P()),
        out_specs=(P("i", None), P("i"), P()),
        check_vma=False,
    )
```

time: 395 us -> 177 us (0.45)
  Pallas kernels: 0 us -> 167 us
  waiting for transfers between devices: 153 us -> 0 us
  starting transfers between devices: 143 us -> 0 us
  blocking collectives: 46.2 us -> 0 us
  matrix products: 16.4 us -> 0 us
  local copies, waits for them, and re-layouts: 19.8 us -> 8.07 us
  between operations: 6.29 us -> 0.64 us
  other arithmetic: 6.11 us -> 1.28 us
    pallas_call x0 -> x1, Pallas kernels: none -> 167 us  [body(): pl.pallas_call(functools.partial(kernel, count), out_shape=(jax.ShapeDtyp...]
    ppermute x8 -> x0, waiting for transfers between devices: 153 us -> none  [passed_along(): lax.ppermute(value, axis, [(source, source + steps) for source in range(i...]
    ppermute x8 -> x0, starting transfers between devices: 143 us -> none  [passed_along(): lax.ppermute(value, axis, [(source, source + steps) for source in range(i...]
    psum x5 -> x0, blocking collectives: 46.2 us -> none  [by_axis(): value = lax.psum(value, axis)]
    dot_general x8 -> x0, matrix products: 16.4 us -> none  [the longest x3 13.6 us: make_tile(): lax.dot_general(left, right, (((0,), (0,)), ((), ())), preferred_element_...]
    unnamed x17 -> x1, local copies, waits for them, and re-layouts: 13.2 us -> 5.62 us
    reduce_sum x3 -> x0, other arithmetic: 4.09 us -> none  [the longest x1 2.22 us: standardize(): column_mean = jnp.mean(values, axis=0)]
  transfers between devices with their start and end apart: 8 -> 0, of which waited for: 3 -> 0; matrix products, arithmetic and copies ran while one was open for 4% -> 0% of each run, Pallas kernels for 0% -> 0%
where the time goes in v1:
time: 177 us
  Pallas kernels  167 us (94%)
  local copies, waits for them, and re-layouts  8.07 us (5%)
    pallas_call x1, Pallas kernels, body(): pl.pallas_call(functools.partial(kernel, count), out_shape=(jax.ShapeDtyp...  167 us
    unnamed x1, local copies, waits for them, and re-layouts  5.62 us

profile of v1, /device:TPU:1, one launch (start us, length us, event | category | flops | bytes accessed | tf_op | source)
XLA Modules:
  0.0 176.8 jit_solution(16059620826704153286)
XLA Ops:
  0.6 1.3 reshape.18.z_ref
  1.9 166.9 %shard_map.58 = (bf16[768,3840]{1,0:T(8,128)(2,1)}, f32[1,768]{1,0:T(1,128)}, f32[8,128]{1,0:T(8,128)}) custom-call(bf16[1536,768]{1,0:T(8,128)(2,1)} %x_hbm.1, f32[1,768]{1,0:T(1,128)} %reshape.18.z_ref, s32[256]{0:T(256)} %reach_ref.1), custom_call_target="tpu_custom_call" | custom-call | tf_op jit(solution)/shard_map/pallas_call | solution.py:332
  168.8 1.2 slice.3
  169.9 1.3 reduce
  171.2 5.6 %copy.7 = bf16[768,3840]{1,0:T(8,128)(2,1)} copy(bf16[768,3840]{1,0:T(8,128)(2,1)} %get-tuple-element.12) | data formatting | bytes 11796480

commit v2 on v1

v2 whole, which is shorter than its diff:
```python
import functools

import jax
import jax.numpy as jnp
from jax import lax
from jax.experimental import pallas as pl
from jax.experimental.pallas import tpu as pltpu
from jax.sharding import Mesh
from jax.sharding import PartitionSpec as P

BAND = 2
MESH = pl.DeviceIdType.MESH
CHUNKS = (256, 256, 128, 128)
ROWS = 256
STEP = 128
WRITES = 6
NT = (((1,), (1,)), ((), ()))

NEAR_STEPS = ((16, 2, "flip"), (32, 2, "flip"), (64, 4, "flip"), (64, 4, "mirror"), (4, 4, "flip"), (4, 4, "mirror"))
STEPS = len(NEAR_STEPS) + 2


def partners_of(me, count):
    partners = []
    for stride, size, kind in NEAR_STEPS:
        digit = lax.rem(lax.div(me, stride), size)
        step = 1 - 2 * lax.rem(digit, 2) if kind == "flip" else size - 1 - 2 * digit
        partners.append(me + step * stride)
    step = 1 - 2 * lax.rem(me, 2)
    partners.append(me + step)
    partners.append(lax.rem(me - step + count, count))
    return partners


def column_stats(source, columns, samples):
    width = columns.size

    def add(step, total):
        rows = pl.ds(pl.multiple_of(step * STEP, STEP), STEP)
        values = source[rows, columns].astype(jnp.float32)
        return total + values.reshape(STEP // 8, 8, width).sum(axis=0)

    zero = jnp.zeros((8, width), jnp.float32)
    total = lax.fori_loop(0, samples // STEP, add, zero)
    mean = jnp.sum(total, axis=0, keepdims=True) / samples

    def add_square(step, total):
        rows = pl.ds(pl.multiple_of(step * STEP, STEP), STEP)
        centered = source[rows, columns].astype(jnp.float32) - mean
        return total + (centered * centered).reshape(STEP // 8, 8, width).sum(axis=0)

    total = lax.fori_loop(0, samples // STEP, add_square, zero)
    variance = jnp.sum(total, axis=0, keepdims=True) / samples
    return mean, lax.rsqrt(variance + 1e-05)


def standardize(source, plain, turned, columns, samples):
    mean, inverse = column_stats(source, columns, samples)

    def write(step, carry):
        rows = pl.ds(pl.multiple_of(step * STEP, STEP), STEP)
        values = (source[rows, columns].astype(jnp.float32) - mean) * inverse
        plain[rows, columns] = values.astype(jnp.bfloat16)
        turned[columns, rows] = values.T.astype(jnp.bfloat16)
        return carry

    lax.fori_loop(0, samples // STEP, write, 0)


def kernel(
    count,
    x_hbm,
    z_hbm,
    reach_hbm,
    out_ref,
    smooth_ref,
    quad_ref,
    own,
    own_scores,
    reach_ref,
    rx,
    plain,
    turned,
    tx,
    left_z,
    right_z,
    own_u,
    near_u,
    tx_smooth,
    rx_smooth,
    partial,
    swapped,
    load_sem,
    send_sem,
    recv_sem,
    z_send,
    z_recv,
    u_send,
    u_recv,
    tile_send,
    tile_recv,
    smooth_send,
    smooth_recv,
    sum_send,
    sum_recv,
):
    me = lax.axis_index("i")
    samples, width = x_hbm.shape
    starts = [sum(CHUNKS[:index]) for index in range(len(CHUNKS))]
    left, right = lax.rem(me + count - 1, count), lax.rem(me + 1, count)
    sides = (left, right)
    partners = partners_of(me, count)

    loads = [
        pltpu.make_async_copy(source, target, load_sem.at[index])
        for index, (source, target) in enumerate(
            ((x_hbm, own), (z_hbm, own_scores), (reach_hbm, reach_ref))
        )
    ]
    for load in loads:
        load.start()
    barrier = pltpu.get_barrier_semaphore()
    peers = sides + tuple(partners[: len(NEAR_STEPS)])
    for device in peers:
        pl.semaphore_signal(barrier, inc=1, device_id=(device,), device_id_type=MESH)
    pl.semaphore_wait(barrier, len(peers))

    def to_side(side, source, target, send, recv):
        return pltpu.make_async_remote_copy(
            src_ref=source,
            dst_ref=target,
            send_sem=send.at[side],
            recv_sem=recv.at[1 - side],
            device_id=(sides[side],),
            device_id_type=MESH,
        )

    def started(copies):
        for copy in copies:
            copy.start()
        return copies

    def chunk_copy(side, chunk):
        columns = pl.ds(starts[chunk], CHUNKS[chunk])
        return pltpu.make_async_remote_copy(
            src_ref=x_hbm.at[:, columns],
            dst_ref=rx.at[1 - side, :, columns],
            send_sem=send_sem.at[side, chunk],
            recv_sem=recv_sem.at[1 - side, chunk],
            device_id=(sides[side],),
            device_id_type=MESH,
        )

    near_z = (left_z, right_z)
    z_copies = started(
        [to_side(side, z_hbm, near_z[1 - side], z_send, z_recv) for side in range(2)]
    )
    chunk_copies = [
        [chunk_copy(side, chunk) for side in range(2)] for chunk in range(len(CHUNKS))
    ]
    started(chunk_copies[0])
    for load in loads:
        load.wait()

    def reach_of(block):
        inside = (block >= 0) & (block < count)
        value = reach_ref[jnp.clip(block, 0, count - 1)]
        return jnp.where(inside, value, -1)

    def factor(first, second, offset):
        allowed = jnp.minimum(reach_of(first), reach_of(second)) >= offset
        return jnp.where(allowed, jnp.float32(1.0), jnp.float32(0.0)) / samples

    near_factor = (factor(me, me - 1, 1), factor(me, me + 1, 1))
    far_factor = factor(me - 1, me + 1, 2)
    own_factor = factor(me, me, 0)

    def as_row(scores):
        return scores[...].astype(jnp.float32).reshape(1, width)

    def as_matrix(scores):
        return jnp.broadcast_to(scores, (8, width)).astype(jnp.bfloat16)

    for start in range(0, width, ROWS):
        standardize(own, plain.at[2], turned.at[2], pl.ds(start, ROWS), samples)
    own_u[...] = jnp.dot(
        as_matrix(as_row(own_scores)), turned[2], preferred_element_type=jnp.float32
    )[0:1, :]

    def into_middle(slot, columns, offset, scale):
        def rows_of(step, carry):
            rows = pl.ds(pl.multiple_of(step * ROWS, ROWS), ROWS)
            product = jnp.dot(
                turned[2, rows, :], plain[slot, :, columns], preferred_element_type=jnp.float32
            )
            place = pl.ds((BAND + offset) * width + columns.start, columns.size)
            out_ref[rows, place] = (product * scale).astype(jnp.bfloat16)
            return carry

        lax.fori_loop(0, width // ROWS, rows_of, 0)

    into_middle(2, pl.ds(0, ROWS), 0, own_factor)
    u_copies = started(
        [to_side(side, own_u, near_u.at[1 - side], u_send, u_recv) for side in range(2)]
    )
    for chunk in range(1, len(CHUNKS) - 1):
        started(chunk_copies[chunk])
    for start in range(ROWS, width, ROWS):
        into_middle(2, pl.ds(start, ROWS), 0, own_factor)

    def sum_copy(step):
        return pltpu.make_async_remote_copy(
            src_ref=partial.at[step],
            dst_ref=swapped.at[step],
            send_sem=sum_send.at[step],
            recv_sem=sum_recv.at[step],
            device_id=(partners[step],),
            device_id_type=MESH,
        )

    sum_copies = [sum_copy(step) for step in range(STEPS)]

    def finish_step(step):
        sum_copies[step].wait_recv()
        partial[step + 1] = partial[step] + swapped[step]

    def tile_copy(side, index, rows, columns):
        place = 2 * BAND * width if side == 0 else 0
        return pltpu.make_async_remote_copy(
            src_ref=tx.at[side, rows, columns],
            dst_ref=out_ref.at[rows, pl.ds(place + columns.start, columns.size)],
            send_sem=tile_send.at[side, index],
            recv_sem=tile_recv.at[1 - side, index],
            device_id=(sides[side],),
            device_id_type=MESH,
        )

    tile_copies = []
    for chunk, (start, size) in enumerate(zip(starts, CHUNKS)):
        columns = pl.ds(start, size)
        for side in range(2):
            chunk_copies[chunk][1 - side].wait_recv()
            standardize(rx.at[side], plain.at[side], turned.at[side], columns, samples)
        pieces = [(columns, pl.ds(0, start + size))]
        if chunk:
            pieces.append((pl.ds(0, start), columns))
        for rows, across in pieces:
            for side in range(2):
                product = jnp.dot(
                    turned[side, rows, :],
                    plain[1 - side, :, across],
                    preferred_element_type=jnp.float32,
                )
                tx[side, rows, across] = (product * far_factor).astype(jnp.bfloat16)
        for side in range(2):
            into_middle(side, columns, 2 * side - 1, near_factor[side])
        if chunk == 0:
            for copy in u_copies:
                copy.wait_recv()
            share = own_u[...] * (own_factor * own_u[...] + 2.0 * near_factor[1] * near_u[1])
            share = share + 2.0 * far_factor * near_u[0] * near_u[1]
            partial[0] = jnp.broadcast_to(jnp.sum(share, axis=1, keepdims=True), (8, 128))
            for step in range(len(NEAR_STEPS)):
                started(sum_copies[step : step + 1])
                finish_step(step)
            started(sum_copies[-2:-1])
            started(chunk_copies[-1])
        tile_copies += started(
            [
                tile_copy(side, 2 * chunk + index, rows, across)
                for index, (rows, across) in enumerate(pieces)
                for side in range(2)
            ]
        )
        if chunk == len(CHUNKS) - 2:
            finish_step(STEPS - 2)
            started(sum_copies[-1:])

    def applied(scores, tile):
        return lax.dot_general(
            as_matrix(scores), tile, NT, preferred_element_type=jnp.float32
        )[0:1, :]

    for copy in z_copies:
        copy.wait_recv()
    near_z = [as_row(scores) for scores in near_z]
    for side in range(2):
        tx_smooth[side] = applied(near_z[1 - side], tx[side])
    row = applied(as_row(own_scores), out_ref[:, pl.ds(BAND * width, width)])
    smooth_copies = started(
        [
            to_side(side, tx_smooth.at[side], rx_smooth.at[1 - side], smooth_send, smooth_recv)
            for side in range(2)
        ]
    )
    for side in range(2):
        place = pl.ds((BAND + 2 * side - 1) * width, width)
        row = row + applied(near_z[side], out_ref[:, place])
    finish_step(STEPS - 1)
    quad_ref[...] = partial[STEPS] / (count * width)
    for copy in smooth_copies:
        copy.wait_recv()
    row = row + rx_smooth[0] + rx_smooth[1]
    smooth_ref[...] = row.reshape(width)
    for copy in tile_copies:
        copy.wait_recv()
    for pair in chunk_copies:
        for copy in pair:
            copy.wait_send()
    for copy in z_copies + u_copies + tile_copies + smooth_copies + sum_copies:
        copy.wait_send()


def finish(tiles_ref, smooth_ref, quad_ref, tiles_hbm, smooth_hbm, quad_out, sems):
    rows = tiles_ref.shape[0] // WRITES
    copies = [pltpu.make_async_copy(smooth_ref, smooth_hbm, sems.at[WRITES])]
    for index in range(WRITES):
        place = pl.ds(index * rows, rows)
        copies.append(
            pltpu.make_async_copy(tiles_ref.at[place], tiles_hbm.at[place], sems.at[index])
        )
    for copy in copies:
        copy.start()
    quad_out[0, 0] = quad_ref[0, 0]
    for copy in copies:
        copy.wait()


def body(count, dosage, zscores, band_reach):
    samples, width = dosage.shape
    chunks = len(CHUNKS)
    bf16, f32 = jnp.bfloat16, jnp.float32
    vmem = pl.BlockSpec(memory_space=pltpu.VMEM)
    hbm = pl.BlockSpec(memory_space=pltpu.HBM)
    smem = pl.BlockSpec(memory_space=pltpu.SMEM)
    placed = pltpu.with_memory_space_constraint
    pair = pltpu.SemaphoreType.DMA((2,))
    results = pl.pallas_call(
        functools.partial(kernel, count),
        out_shape=(
            pltpu.VMEM((width, (2 * BAND + 1) * width), bf16),
            pltpu.VMEM((width,), f32),
            pltpu.VMEM((8, 128), f32),
        ),
        in_specs=[hbm, hbm, hbm],
        out_specs=(vmem, vmem, vmem),
        scratch_shapes=[
            pltpu.VMEM((samples, width), bf16),
            pltpu.VMEM((width,), bf16),
            pltpu.SMEM((count,), jnp.int32),
            pltpu.VMEM((2, samples, width), bf16),
            pltpu.VMEM((3, samples, width), bf16),
            pltpu.VMEM((3, width, samples), bf16),
            pltpu.VMEM((2, width, width), bf16),
            pltpu.VMEM((width,), bf16),
            pltpu.VMEM((width,), bf16),
            pltpu.VMEM((1, samples), f32),
            pltpu.VMEM((2, 1, samples), f32),
            pltpu.VMEM((2, 1, width), f32),
            pltpu.VMEM((2, 1, width), f32),
            pltpu.VMEM((STEPS + 1, 8, 128), f32),
            pltpu.VMEM((STEPS, 8, 128), f32),
            pltpu.SemaphoreType.DMA((3,)),
            pltpu.SemaphoreType.DMA((2, chunks)),
            pltpu.SemaphoreType.DMA((2, chunks)),
            pair,
            pair,
            pair,
            pair,
            pltpu.SemaphoreType.DMA((2, 2 * chunks)),
            pltpu.SemaphoreType.DMA((2, 2 * chunks)),
            pair,
            pair,
            pltpu.SemaphoreType.DMA((STEPS,)),
            pltpu.SemaphoreType.DMA((STEPS,)),
        ],
        compiler_params=pltpu.CompilerParams(
            collective_id=0, has_side_effects=True, vmem_limit_bytes=40 * 1024 * 1024
        ),
    )(*[placed(value, pltpu.HBM) for value in (dosage, zscores, band_reach)])
    ld_tiles, smoothed, quadratic = pl.pallas_call(
        finish,
        out_shape=(
            jax.ShapeDtypeStruct((width, (2 * BAND + 1) * width), bf16),
            jax.ShapeDtypeStruct((width,), f32),
            jax.ShapeDtypeStruct((1, 1), f32),
        ),
        in_specs=[vmem, vmem, vmem],
        out_specs=(hbm, hbm, smem),
        scratch_shapes=[pltpu.SemaphoreType.DMA((WRITES + 1,))],
        compiler_params=pltpu.CompilerParams(vmem_limit_bytes=1024 * 1024),
    )(*[placed(value, pltpu.VMEM) for value in results])
    return ld_tiles, smoothed, quadratic[0, 0]


def solution(mesh):
    count = mesh.devices.size
    line = Mesh(mesh.devices.reshape(count), ("i",))
    return jax.shard_map(
        functools.partial(body, count),
        mesh=line,
        in_specs=(P(None, "i"), P("i"), P()),
        out_specs=(P("i", None), P("i"), P()),
        check_vma=False,
    )
```

time: 177 us -> 179 us (1.011)
  Pallas kernels: 167 us -> 178 us
  local copies, waits for them, and re-layouts: 8.07 us -> 0 us
    pallas_call x1 -> x2, Pallas kernels: 167 us -> 178 us  [the longest x1 175 us: body(): pl.pallas_call(functools.partial(kernel, count), out_shape=(pltpu.VMEM((w...]
    unnamed x1 -> x0, local copies, waits for them, and re-layouts: 5.62 us -> none
where the time goes in v2:
time: 179 us
  Pallas kernels  178 us (99%)
    pallas_call x1, Pallas kernels, body(): pl.pallas_call(functools.partial(kernel, count), out_shape=(pltpu.VMEM((w...  175 us

profile of v2, /device:TPU:1, one launch (start us, length us, event | category | flops | bytes accessed | tf_op | source)
XLA Modules:
  0.0 178.6 jit_solution(12343858279108283482)
XLA Ops:
  0.6 174.8 %shard_map.58 = (bf16[768,3840]{1,0:T(8,128)(2,1)S(1)}, f32[768]{0:T(1024)S(1)}, f32[8,128]{1,0:T(8,128)S(1)}) custom-call(bf16[1536,768]{1,0:T(8,128)(2,1)} %x_hbm.1, bf16[768]{0:T(1024)(128)(2,1)} %z_hbm.1, s32[256]{0:T(256)} %reach_hbm.1), custom_call_target="tpu_custom_call" | custom-call | tf_op jit(solution)/shard_map/pallas_call | solution.py:338
  175.5 3.1 %shard_map.59 = (bf16[768,3840]{1,0:T(8,128)(2,1)}, f32[768]{0:T(1024)}, f32[1,1]{1,0:T(1,128)}) custom-call(bf16[768,3840]{1,0:T(8,128)(2,1)S(1)} %get-tuple-element.9.tiles_ref, f32[768]{0:T(1024)S(1)} %get-tuple-element.10.smooth_ref, f32[8,128]{1,0:T(8,128)S(1)} %get-tuple-element.11.quad_ref), custom_call_target="tpu_custom_call" | custom-call | tf_op jit(solution)/shard_map/pallas_call | solution.py:381

commit v3 on v2

--- a/solution.py
+++ b/solution.py
@@ -16,7 +16,7 @@
 WRITES = 6
 NT = (((1,), (1,)), ((), ()))
 
-NEAR_STEPS = ((16, 2, "flip"), (32, 2, "flip"), (64, 4, "flip"), (64, 4, "mirror"), (4, 4, "flip"), (4, 4, "mirror"))
+NEAR_STEPS = ((16, 2, "flip"), (64, 4, "flip"), (64, 4, "mirror"), (4, 4, "flip"), (4, 4, "mirror"), (32, 2, "flip"))
 STEPS = len(NEAR_STEPS) + 2
 
 
@@ -203,8 +203,8 @@
     u_copies = started(
         [to_side(side, own_u, near_u.at[1 - side], u_send, u_recv) for side in range(2)]
     )
-    for chunk in range(1, len(CHUNKS) - 1):
-        started(chunk_copies[chunk])
+    for copies in chunk_copies[1:-1]:
+        started(copies)
     for start in range(ROWS, width, ROWS):
         into_middle(2, pl.ds(start, ROWS), 0, own_factor)
 
@@ -236,10 +236,16 @@
         )
 
     tile_copies = []
+    ready = []
     for chunk, (start, size) in enumerate(zip(starts, CHUNKS)):
         columns = pl.ds(start, size)
         for side in range(2):
             chunk_copies[chunk][1 - side].wait_recv()
+            if side == 1 and chunk == len(CHUNKS) - 2:
+                finish_step(STEPS - 3)
+                started(sum_copies[STEPS - 2 : STEPS - 1])
+                tile_copies += started(ready)
+                ready = []
             standardize(rx.at[side], plain.at[side], turned.at[side], columns, samples)
         pieces = [(columns, pl.ds(0, start + size))]
         if chunk:
@@ -252,29 +258,30 @@
                     preferred_element_type=jnp.float32,
                 )
                 tx[side, rows, across] = (product * far_factor).astype(jnp.bfloat16)
-        for side in range(2):
-            into_middle(side, columns, 2 * side - 1, near_factor[side])
+        ready += [
+            tile_copy(side, 2 * chunk + index, rows, across)
+            for index, (rows, across) in enumerate(pieces)
+            for side in range(2)
+        ]
+        if chunk < len(CHUNKS) - 1:
+            for side in range(2):
+                into_middle(side, columns, 2 * side - 1, near_factor[side])
         if chunk == 0:
             for copy in u_copies:
                 copy.wait_recv()
             share = own_u[...] * (own_factor * own_u[...] + 2.0 * near_factor[1] * near_u[1])
             share = share + 2.0 * far_factor * near_u[0] * near_u[1]
             partial[0] = jnp.broadcast_to(jnp.sum(share, axis=1, keepdims=True), (8, 128))
-            for step in range(len(NEAR_STEPS)):
+            for step in range(STEPS - 3):
                 started(sum_copies[step : step + 1])
                 finish_step(step)
-            started(sum_copies[-2:-1])
+            started(sum_copies[STEPS - 3 : STEPS - 2])
             started(chunk_copies[-1])
-        tile_copies += started(
-            [
-                tile_copy(side, 2 * chunk + index, rows, across)
-                for index, (rows, across) in enumerate(pieces)
-                for side in range(2)
-            ]
-        )
         if chunk == len(CHUNKS) - 2:
             finish_step(STEPS - 2)
-            started(sum_copies[-1:])
+            started(sum_copies[STEPS - 1 :])
+            tile_copies += started(ready)
+            ready = []
 
     def applied(scores, tile):
         return lax.dot_general(
@@ -286,14 +293,16 @@
     near_z = [as_row(scores) for scores in near_z]
     for side in range(2):
         tx_smooth[side] = applied(near_z[1 - side], tx[side])
-    row = applied(as_row(own_scores), out_ref[:, pl.ds(BAND * width, width)])
     smooth_copies = started(
         [
             to_side(side, tx_smooth.at[side], rx_smooth.at[1 - side], smooth_send, smooth_recv)
             for side in range(2)
         ]
     )
+    tile_copies += started(ready)
+    row = applied(as_row(own_scores), out_ref[:, pl.ds(BAND * width, width)])
     for side in range(2):
+        into_middle(side, columns, 2 * side - 1, near_factor[side])
         place = pl.ds((BAND + 2 * side - 1) * width, width)
         row = row + applied(near_z[side], out_ref[:, place])
     finish_step(STEPS - 1)

time: 179 us -> 172 us (0.961); the launches traced: 179 us -> 169 us
  Pallas kernels: 178 us -> 169 us
    pallas_call x1, Pallas kernels: 175 us -> 166 us  [body(): pl.pallas_call(functools.partial(kernel, count), out_shape=(pltpu.VMEM((w...]
where the time goes in v3:
time: 172 us; the launch traced here: 169 us
  Pallas kernels  169 us (98%)
    pallas_call x1, Pallas kernels, body(): pl.pallas_call(functools.partial(kernel, count), out_shape=(pltpu.VMEM((w...  166 us

profile of v3, /device:TPU:1, one launch (start us, length us, event | category | flops | bytes accessed | tf_op | source)
XLA Modules:
  0.0 169.4 jit_solution(14614553922229383336)
XLA Ops:
  0.6 165.6 %shard_map.58 = (bf16[768,3840]{1,0:T(8,128)(2,1)S(1)}, f32[768]{0:T(1024)S(1)}, f32[8,128]{1,0:T(8,128)S(1)}) custom-call(bf16[1536,768]{1,0:T(8,128)(2,1)} %x_hbm.1, bf16[768]{0:T(1024)(128)(2,1)} %z_hbm.1, s32[256]{0:T(256)} %reach_hbm.1), custom_call_target="tpu_custom_call" | custom-call | tf_op jit(solution)/shard_map/pallas_call | solution.py:347
  166.3 3.1 %shard_map.59 = (bf16[768,3840]{1,0:T(8,128)(2,1)}, f32[768]{0:T(1024)}, f32[1,1]{1,0:T(1,128)}) custom-call(bf16[768,3840]{1,0:T(8,128)(2,1)S(1)} %get-tuple-element.9.tiles_ref, f32[768]{0:T(1024)S(1)} %get-tuple-element.10.smooth_ref, f32[8,128]{1,0:T(8,128)S(1)} %get-tuple-element.11.quad_ref), custom_call_target="tpu_custom_call" | custom-call | tf_op jit(solution)/shard_map/pallas_call | solution.py:390

commit v4 on v3

--- a/solution.py
+++ b/solution.py
@@ -203,8 +203,7 @@
     u_copies = started(
         [to_side(side, own_u, near_u.at[1 - side], u_send, u_recv) for side in range(2)]
     )
-    for copies in chunk_copies[1:-1]:
-        started(copies)
+    started(chunk_copies[1])
     for start in range(ROWS, width, ROWS):
         into_middle(2, pl.ds(start, ROWS), 0, own_factor)
 
@@ -241,11 +240,8 @@
         columns = pl.ds(start, size)
         for side in range(2):
             chunk_copies[chunk][1 - side].wait_recv()
-            if side == 1 and chunk == len(CHUNKS) - 2:
-                finish_step(STEPS - 3)
-                started(sum_copies[STEPS - 2 : STEPS - 1])
-                tile_copies += started(ready)
-                ready = []
+            if chunk < 2 and side == 1:
+                started(chunk_copies[chunk + 2])
             standardize(rx.at[side], plain.at[side], turned.at[side], columns, samples)
         pieces = [(columns, pl.ds(0, start + size))]
         if chunk:
@@ -276,10 +272,10 @@
                 started(sum_copies[step : step + 1])
                 finish_step(step)
             started(sum_copies[STEPS - 3 : STEPS - 2])
-            started(chunk_copies[-1])
         if chunk == len(CHUNKS) - 2:
-            finish_step(STEPS - 2)
-            started(sum_copies[STEPS - 1 :])
+            finish_step(STEPS - 3)
+            started(sum_copies[STEPS - 2 : STEPS - 1])
+        if chunk < len(CHUNKS) - 1:
             tile_copies += started(ready)
             ready = []
 
@@ -299,7 +295,12 @@
             for side in range(2)
         ]
     )
-    tile_copies += started(ready)
+    for copy in tile_copies[:6]:
+        copy.wait_recv()
+    tile_copies += started(ready[:2])
+    finish_step(STEPS - 2)
+    started(sum_copies[STEPS - 1 :])
+    tile_copies += started(ready[2:])
     row = applied(as_row(own_scores), out_ref[:, pl.ds(BAND * width, width)])
     for side in range(2):
         into_middle(side, columns, 2 * side - 1, near_factor[side])
@@ -311,7 +312,7 @@
         copy.wait_recv()
     row = row + rx_smooth[0] + rx_smooth[1]
     smooth_ref[...] = row.reshape(width)
-    for copy in tile_copies:
+    for copy in tile_copies[6:]:
         copy.wait_recv()
     for pair in chunk_copies:
         for copy in pair:
@@ -320,17 +321,20 @@
         copy.wait_send()
 
 
-def finish(tiles_ref, smooth_ref, quad_ref, tiles_hbm, smooth_hbm, quad_out, sems):
+def finish(tiles_ref, smooth_ref, quad_ref, tiles_hbm, smooth_hbm, quad_hbm, quad, sems):
     rows = tiles_ref.shape[0] // WRITES
-    copies = [pltpu.make_async_copy(smooth_ref, smooth_hbm, sems.at[WRITES])]
+    copies = []
     for index in range(WRITES):
         place = pl.ds(index * rows, rows)
         copies.append(
             pltpu.make_async_copy(tiles_ref.at[place], tiles_hbm.at[place], sems.at[index])
         )
-    for copy in copies:
+    copies.append(pltpu.make_async_copy(smooth_ref, smooth_hbm, sems.at[WRITES]))
+    copies.append(pltpu.make_async_copy(quad, quad_hbm, sems.at[WRITES + 1]))
+    for copy in copies[:-1]:
         copy.start()
-    quad_out[0, 0] = quad_ref[0, 0]
+    quad[0, 0] = quad_ref[0, 0]
+    copies[-1].start()
     for copy in copies:
         copy.wait()
 
@@ -341,7 +345,6 @@
     bf16, f32 = jnp.bfloat16, jnp.float32
     vmem = pl.BlockSpec(memory_space=pltpu.VMEM)
     hbm = pl.BlockSpec(memory_space=pltpu.HBM)
-    smem = pl.BlockSpec(memory_space=pltpu.SMEM)
     placed = pltpu.with_memory_space_constraint
     pair = pltpu.SemaphoreType.DMA((2,))
     results = pl.pallas_call(
@@ -395,8 +398,8 @@
             jax.ShapeDtypeStruct((1, 1), f32),
         ),
         in_specs=[vmem, vmem, vmem],
-        out_specs=(hbm, hbm, smem),
-        scratch_shapes=[pltpu.SemaphoreType.DMA((WRITES + 1,))],
+        out_specs=(hbm, hbm, hbm),
+        scratch_shapes=[pltpu.SMEM((1, 1), f32), pltpu.SemaphoreType.DMA((WRITES + 2,))],
         compiler_params=pltpu.CompilerParams(vmem_limit_bytes=1024 * 1024),
     )(*[placed(value, pltpu.VMEM) for value in results])
     return ld_tiles, smoothed, quadratic[0, 0]

time: 172 us -> 170 us (0.988)
  no operation moved by 1% of the time
where the time goes in v4:
time: 170 us; the launch traced here: 169 us
  Pallas kernels  168 us (99%)
    pallas_call x1, Pallas kernels, body(): pl.pallas_call(functools.partial(kernel, count), out_shape=(pltpu.VMEM((w...  166 us

profile of v4, /device:TPU:1, one launch (start us, length us, event | category | flops | bytes accessed | tf_op | source)
XLA Modules:
  0.0 168.9 jit_solution(13322257271582477693)
XLA Ops:
  0.6 165.6 %shard_map.58 = (bf16[768,3840]{1,0:T(8,128)(2,1)S(1)}, f32[768]{0:T(1024)S(1)}, f32[8,128]{1,0:T(8,128)S(1)}) custom-call(bf16[1536,768]{1,0:T(8,128)(2,1)} %x_hbm.1, bf16[768]{0:T(1024)(128)(2,1)} %z_hbm.1, s32[256]{0:T(256)} %reach_hbm.1), custom_call_target="tpu_custom_call" | custom-call | tf_op jit(solution)/shard_map/pallas_call | solution.py:350
  166.3 2.6 %shard_map.59 = (bf16[768,3840]{1,0:T(8,128)(2,1)}, f32[768]{0:T(1024)}, f32[1,1]{1,0:T(1,128)}) custom-call(bf16[768,3840]{1,0:T(8,128)(2,1)S(1)} %get-tuple-element.9.tiles_ref, f32[768]{0:T(1024)S(1)} %get-tuple-element.10.smooth_ref, f32[8,128]{1,0:T(8,128)S(1)} %get-tuple-element.11.quad_ref), custom_call_target="tpu_custom_call" | custom-call | tf_op jit(solution)/shard_map/pallas_call | solution.py:393

commit v5 on v4

--- a/solution.py
+++ b/solution.py
@@ -295,8 +295,6 @@
             for side in range(2)
         ]
     )
-    for copy in tile_copies[:6]:
-        copy.wait_recv()
     tile_copies += started(ready[:2])
     finish_step(STEPS - 2)
     started(sum_copies[STEPS - 1 :])
@@ -312,7 +310,7 @@
         copy.wait_recv()
     row = row + rx_smooth[0] + rx_smooth[1]
     smooth_ref[...] = row.reshape(width)
-    for copy in tile_copies[6:]:
+    for copy in tile_copies:
         copy.wait_recv()
     for pair in chunk_copies:
         for copy in pair:

time: 170 us -> 170 us (level)
  no operation moved by 1% of the time
where the time goes in v5:
time: 170 us; the launch traced here: 169 us
  Pallas kernels  168 us (99%)
    pallas_call x1, Pallas kernels, body(): pl.pallas_call(functools.partial(kernel, count), out_shape=(pltpu.VMEM((w...  166 us

profile of v5, /device:TPU:1, one launch (start us, length us, event | category | flops | bytes accessed | tf_op | source)
XLA Modules:
  0.0 168.9 jit_solution(6846771095119238384)
XLA Ops:
  0.6 165.6 %shard_map.58 = (bf16[768,3840]{1,0:T(8,128)(2,1)S(1)}, f32[768]{0:T(1024)S(1)}, f32[8,128]{1,0:T(8,128)S(1)}) custom-call(bf16[1536,768]{1,0:T(8,128)(2,1)} %x_hbm.1, bf16[768]{0:T(1024)(128)(2,1)} %z_hbm.1, s32[256]{0:T(256)} %reach_hbm.1), custom_call_target="tpu_custom_call" | custom-call | tf_op jit(solution)/shard_map/pallas_call | solution.py:348
  166.3 2.6 %shard_map.59 = (bf16[768,3840]{1,0:T(8,128)(2,1)}, f32[768]{0:T(1024)}, f32[1,1]{1,0:T(1,128)}) custom-call(bf16[768,3840]{1,0:T(8,128)(2,1)S(1)} %get-tuple-element.9.tiles_ref, f32[768]{0:T(1024)S(1)} %get-tuple-element.10.smooth_ref, f32[8,128]{1,0:T(8,128)S(1)} %get-tuple-element.11.quad_ref), custom_call_target="tpu_custom_call" | custom-call | tf_op jit(solution)/shard_map/pallas_call | solution.py:391

commit v6 on v5

--- a/solution.py
+++ b/solution.py
@@ -84,6 +84,7 @@
     tx,
     left_z,
     right_z,
+    own_row,
     own_u,
     near_u,
     tx_smooth,
@@ -206,6 +207,13 @@
     started(chunk_copies[1])
     for start in range(ROWS, width, ROWS):
         into_middle(2, pl.ds(start, ROWS), 0, own_factor)
+
+    def applied(scores, tile):
+        return lax.dot_general(
+            as_matrix(scores), tile, NT, preferred_element_type=jnp.float32
+        )[0:1, :]
+
+    own_row[...] = applied(as_row(own_scores), out_ref[:, pl.ds(BAND * width, width)])
 
     def sum_copy(step):
         return pltpu.make_async_remote_copy(
@@ -265,9 +273,10 @@
         if chunk == 0:
             for copy in u_copies:
                 copy.wait_recv()
-            share = own_u[...] * (own_factor * own_u[...] + 2.0 * near_factor[1] * near_u[1])
-            share = share + 2.0 * far_factor * near_u[0] * near_u[1]
-            partial[0] = jnp.broadcast_to(jnp.sum(share, axis=1, keepdims=True), (8, 128))
+            share = near_factor[1] * own_u[...] * near_u[1] + far_factor * near_u[0] * near_u[1]
+            total = 2.0 * jnp.sum(share, axis=1, keepdims=True)
+            total = total + jnp.sum(as_row(own_scores) * own_row[...], axis=1, keepdims=True)
+            partial[0] = jnp.broadcast_to(total, (8, 128))
             for step in range(STEPS - 3):
                 started(sum_copies[step : step + 1])
                 finish_step(step)
@@ -278,11 +287,6 @@
         if chunk < len(CHUNKS) - 1:
             tile_copies += started(ready)
             ready = []
-
-    def applied(scores, tile):
-        return lax.dot_general(
-            as_matrix(scores), tile, NT, preferred_element_type=jnp.float32
-        )[0:1, :]
 
     for copy in z_copies:
         copy.wait_recv()
@@ -299,7 +303,7 @@
     finish_step(STEPS - 2)
     started(sum_copies[STEPS - 1 :])
     tile_copies += started(ready[2:])
-    row = applied(as_row(own_scores), out_ref[:, pl.ds(BAND * width, width)])
+    row = own_row[...]
     for side in range(2):
         into_middle(side, columns, 2 * side - 1, near_factor[side])
         place = pl.ds((BAND + 2 * side - 1) * width, width)
@@ -364,6 +368,7 @@
             pltpu.VMEM((2, width, width), bf16),
             pltpu.VMEM((width,), bf16),
             pltpu.VMEM((width,), bf16),
+            pltpu.VMEM((1, width), f32),
             pltpu.VMEM((1, samples), f32),
             pltpu.VMEM((2, 1, samples), f32),
             pltpu.VMEM((2, 1, width), f32),

time: 170 us -> 170 us (level)
  no operation moved by 1% of the time
where the time goes in v6:
time: 170 us; the launch traced here: 169 us
  Pallas kernels  168 us (99%)
    pallas_call x1, Pallas kernels, body(): pl.pallas_call(functools.partial(kernel, count), out_shape=(pltpu.VMEM((w...  166 us

profile of v6, /device:TPU:1, one launch (start us, length us, event | category | flops | bytes accessed | tf_op | source)
XLA Modules:
  0.0 168.9 jit_solution(9315678790365537557)
XLA Ops:
  0.6 165.6 %shard_map.58 = (bf16[768,3840]{1,0:T(8,128)(2,1)S(1)}, f32[768]{0:T(1024)S(1)}, f32[8,128]{1,0:T(8,128)S(1)}) custom-call(bf16[1536,768]{1,0:T(8,128)(2,1)} %x_hbm.1, bf16[768]{0:T(1024)(128)(2,1)} %z_hbm.1, s32[256]{0:T(256)} %reach_hbm.1), custom_call_target="tpu_custom_call" | custom-call | tf_op jit(solution)/shard_map/pallas_call | solution.py:352
  166.3 2.6 %shard_map.59 = (bf16[768,3840]{1,0:T(8,128)(2,1)}, f32[768]{0:T(1024)}, f32[1,1]{1,0:T(1,128)}) custom-call(bf16[768,3840]{1,0:T(8,128)(2,1)S(1)} %get-tuple-element.9.tiles_ref, f32[768]{0:T(1024)S(1)} %get-tuple-element.10.smooth_ref, f32[8,128]{1,0:T(8,128)S(1)} %get-tuple-element.11.quad_ref), custom_call_target="tpu_custom_call" | custom-call | tf_op jit(solution)/shard_map/pallas_call | solution.py:396

commit v7 on v6

--- a/solution.py
+++ b/solution.py
@@ -277,7 +277,10 @@
             total = 2.0 * jnp.sum(share, axis=1, keepdims=True)
             total = total + jnp.sum(as_row(own_scores) * own_row[...], axis=1, keepdims=True)
             partial[0] = jnp.broadcast_to(total, (8, 128))
-            for step in range(STEPS - 3):
+            started(sum_copies[:1])
+        if chunk == 1:
+            finish_step(0)
+            for step in range(1, STEPS - 3):
                 started(sum_copies[step : step + 1])
                 finish_step(step)
             started(sum_copies[STEPS - 3 : STEPS - 2])

time: 170 us -> 169 us (level)
  no operation moved by 1% of the time
where the time goes in v7:
time: 169 us
  Pallas kernels  168 us (99%)
    pallas_call x1, Pallas kernels, body(): pl.pallas_call(functools.partial(kernel, count), out_shape=(pltpu.VMEM((w...  166 us

profile of v7, /device:TPU:1, one launch (start us, length us, event | category | flops | bytes accessed | tf_op | source)
XLA Modules:
  0.0 168.9 jit_solution(7917218696864120248)
XLA Ops:
  0.6 165.6 %shard_map.58 = (bf16[768,3840]{1,0:T(8,128)(2,1)S(1)}, f32[768]{0:T(1024)S(1)}, f32[8,128]{1,0:T(8,128)S(1)}) custom-call(bf16[1536,768]{1,0:T(8,128)(2,1)} %x_hbm.1, bf16[768]{0:T(1024)(128)(2,1)} %z_hbm.1, s32[256]{0:T(256)} %reach_hbm.1), custom_call_target="tpu_custom_call" | custom-call | tf_op jit(solution)/shard_map/pallas_call | solution.py:355
  166.3 2.6 %shard_map.59 = (bf16[768,3840]{1,0:T(8,128)(2,1)}, f32[768]{0:T(1024)}, f32[1,1]{1,0:T(1,128)}) custom-call(bf16[768,3840]{1,0:T(8,128)(2,1)S(1)} %get-tuple-element.9.tiles_ref, f32[768]{0:T(1024)S(1)} %get-tuple-element.10.smooth_ref, f32[8,128]{1,0:T(8,128)S(1)} %get-tuple-element.11.quad_ref), custom_call_target="tpu_custom_call" | custom-call | tf_op jit(solution)/shard_map/pallas_call | solution.py:399

commit v8 on v6

--- a/solution.py
+++ b/solution.py
@@ -277,16 +277,19 @@
             total = 2.0 * jnp.sum(share, axis=1, keepdims=True)
             total = total + jnp.sum(as_row(own_scores) * own_row[...], axis=1, keepdims=True)
             partial[0] = jnp.broadcast_to(total, (8, 128))
-            for step in range(STEPS - 3):
-                started(sum_copies[step : step + 1])
-                finish_step(step)
-            started(sum_copies[STEPS - 3 : STEPS - 2])
+            started(sum_copies[:1])
         if chunk == len(CHUNKS) - 2:
             finish_step(STEPS - 3)
             started(sum_copies[STEPS - 2 : STEPS - 1])
         if chunk < len(CHUNKS) - 1:
             tile_copies += started(ready)
             ready = []
+        if chunk == 0:
+            finish_step(0)
+            for step in range(1, STEPS - 3):
+                started(sum_copies[step : step + 1])
+                finish_step(step)
+            started(sum_copies[STEPS - 3 : STEPS - 2])
 
     for copy in z_copies:
         copy.wait_recv()

time: 170 us -> 171 us (level)
  no operation moved by 1% of the time
where the time goes in v8:
time: 171 us; the launch traced here: 169 us
  Pallas kernels  168 us (98%)
    pallas_call x1, Pallas kernels, body(): pl.pallas_call(functools.partial(kernel, count), out_shape=(pltpu.VMEM((w...  166 us

profile of v8, /device:TPU:1, one launch (start us, length us, event | category | flops | bytes accessed | tf_op | source)
XLA Modules:
  0.0 168.9 jit_solution(16761523239447959013)
XLA Ops:
  0.6 165.6 %shard_map.58 = (bf16[768,3840]{1,0:T(8,128)(2,1)S(1)}, f32[768]{0:T(1024)S(1)}, f32[8,128]{1,0:T(8,128)S(1)}) custom-call(bf16[1536,768]{1,0:T(8,128)(2,1)} %x_hbm.1, bf16[768]{0:T(1024)(128)(2,1)} %z_hbm.1, s32[256]{0:T(256)} %reach_hbm.1), custom_call_target="tpu_custom_call" | custom-call | tf_op jit(solution)/shard_map/pallas_call | solution.py:355
  166.3 2.6 %shard_map.59 = (bf16[768,3840]{1,0:T(8,128)(2,1)}, f32[768]{0:T(1024)}, f32[1,1]{1,0:T(1,128)}) custom-call(bf16[768,3840]{1,0:T(8,128)(2,1)S(1)} %get-tuple-element.9.tiles_ref, f32[768]{0:T(1024)S(1)} %get-tuple-element.10.smooth_ref, f32[8,128]{1,0:T(8,128)S(1)} %get-tuple-element.11.quad_ref), custom_call_target="tpu_custom_call" | custom-call | tf_op jit(solution)/shard_map/pallas_call | solution.py:399
